TPU v7x, 32 devices: a whole 2x2x4 slice. The times are simulated.
32 devices in a mesh: groups: 2 (over x), seq: 8 (over z, y), mp: 2 (over core).
Axes of the slice: x: 2, y: 2, z: 4, core: 2. Of those that a mesh axis runs over, the one named last changes fastest.
Arguments:
- latent_cache: bfloat16 [2048, 64, 512], P(('groups', 'seq')), parts along dimension 0, may hold values from -6 to 6
- rope_cache: bfloat16 [2048, 4096], P(('groups', 'seq')), parts along dimension 0, may hold values from -6 to 6
- q_nope: bfloat16 [16, 128, 128], P('groups', 'mp'), parts along dimension 0, may hold values from -12 to 12
- q_rope: bfloat16 [16, 128, 64], P('groups', 'mp'), parts along dimension 0, may hold values from -2000 to 2000
- w_uk: bfloat16 [128, 128, 512], P('mp', None, 'seq'), may hold values from -0.5 to 0.5
- value_up_weight: bfloat16 [128, 512, 128], P('mp', 'seq'), may hold values from -0.25 to 0.25
- w_out: bfloat16 [16384, 7168], P('mp', 'seq'), may hold values from -0.046875 to 0.046875
- page_table: int32 [16, 256], P('groups'), parts along dimension 0, may hold values from 0 to 1023, as said below
- lengths: int32 [16], P('groups'), parts along dimension 0, may hold values from 2048 to 16384, as said below
Outputs:
- output: bfloat16 [16, 7168], P('groups', ('seq', 'mp')), parts along dimension 0
There are 2 independent parts, one for each index of `groups`. A program takes and returns all parts, laid end to end along the dimension named above; an argument that names none is the same for every part. Nothing has to cross between parts.
Inputs may be any that keep to these rules, and one draw needn't show every extreme that they name: `lengths`: every sequence has one eighth of 16384 tokens or more; the longest has exactly 16384. page_table[b,p] for p < ceil(lengths[b] / 64) is the global slot (shard index times 128 plus local slot) holding that page; these live entries are all distinct; the other entries are 0 and unused.
All inputs are finite; a program needn't handle non-finite values.
Results may differ from a plain program's by a relative error of at most 0.012.
Values may be sent and summed in bfloat16 or wider, within the bound.
A program may use at most 128 MiB of HBM per device.

v0:
```python
import jax
import jax.numpy as jnp
from jax import lax
from jax.sharding import PartitionSpec as P

NEG = -1e30


def local(
    latent_cache, rope_cache, q_nope, q_rope, w_uk, value_up_weight, w_out, page_table, lengths
):
    peak_score = lax.Precision.HIGHEST
    slots_dev, page_len, latent_width = latent_cache.shape
    rope_width = q_rope.shape[2]
    seq_count, heads = (q_nope.shape[0], q_nope.shape[1])
    score_scale = (q_nope.shape[2] + rope_width) ** (-0.5)
    q_part = jnp.einsum("bhn,hnk->bhk", q_nope, w_uk, preferred_element_type=jnp.float32).astype(
        jnp.bfloat16
    )
    q_latent = lax.all_gather(q_part, "seq", axis=2, tiled=True)
    first_slot = lax.axis_index("seq") * slots_dev
    page_count = (lengths + page_len - 1) // page_len
    logical = jnp.arange(page_table.shape[1], dtype=jnp.int32)
    live_page = logical[None, :] < page_count[:, None]
    tokens_in = jnp.clip(lengths[:, None] - page_len * logical[None, :], 0, page_len)
    local_ids = jnp.arange(slots_dev, dtype=jnp.int32)
    hits = ((page_table - first_slot)[:, :, None] == local_ids[None, None, :]) & live_page[
        :, :, None
    ]
    owner_mask = jnp.any(hits, axis=1)
    slot_fill = jnp.sum(jnp.where(hits, tokens_in[:, :, None], 0), axis=(0, 1))
    owner_half = owner_mask.astype(jnp.bfloat16)

    def update(run_state, index):
        run_max, run_sum, run_out = run_state
        start = index * 8
        latent_block = lax.dynamic_slice_in_dim(latent_cache, start, 8, 0)
        rope_block = lax.dynamic_slice_in_dim(rope_cache, start, 8, 0).reshape(
            8, page_len, rope_width
        )
        owner_block = lax.dynamic_slice_in_dim(owner_half, start, 8, 1)
        fill_block = lax.dynamic_slice_in_dim(slot_fill, start, 8, 0)
        pick_latent = jnp.einsum(
            "bs,bhk->shk", owner_block, q_latent, preferred_element_type=jnp.float32
        ).astype(jnp.bfloat16)
        pick_rope = jnp.einsum(
            "bs,bhr->shr", owner_block, q_rope, preferred_element_type=jnp.float32
        ).astype(jnp.bfloat16)
        scores = (
            jnp.einsum(
                "shk,stk->sht", pick_latent, latent_block, preferred_element_type=jnp.float32
            )
            + jnp.einsum("shr,str->sht", pick_rope, rope_block, preferred_element_type=jnp.float32)
        ) * score_scale
        live_token = (
            jnp.arange(page_len, dtype=jnp.int32)[None, None, :] < fill_block[:, None, None]
        )
        slot_max = jnp.max(jnp.where(live_token, scores, NEG), axis=2)
        exponent = jnp.where(live_token, jnp.exp(scores - slot_max[:, :, None]), 0.0)
        slot_sum = jnp.sum(exponent, axis=2)
        slot_out = jnp.einsum(
            "sht,stk->shk",
            exponent.astype(jnp.bfloat16),
            latent_block,
            preferred_element_type=jnp.float32,
        )
        owned = owner_block > 0
        candidate = jnp.where(owned[:, :, None], slot_max[None, :, :], NEG)
        new_max = jnp.maximum(run_max, jnp.max(candidate, axis=1))
        carry_scale = jnp.exp(run_max - new_max)
        factor = jnp.where(owned[:, :, None], jnp.exp(candidate - new_max[:, None, :]), 0.0)
        run_sum = run_sum * carry_scale + jnp.einsum(
            "bsh,sh->bh", factor, slot_sum, precision=peak_score
        )
        run_out = run_out * carry_scale[:, :, None] + jnp.einsum(
            "bsh,shk->bhk", factor, slot_out, precision=peak_score
        )
        return (new_max, run_sum, run_out)

    def visit(index, run_state):
        return update(run_state, index)

    initial = (
        jnp.full((seq_count, heads), NEG, jnp.float32),
        jnp.zeros((seq_count, heads), jnp.float32),
        jnp.zeros((seq_count, heads, latent_width), jnp.float32),
    )
    run_max, run_sum, run_out = lax.fori_loop(0, slots_dev // 8, visit, initial)
    share_width = value_up_weight.shape[1]
    shards = lax.axis_size("seq")
    spread_max = jnp.broadcast_to(run_max[:, :, None], (seq_count, heads, shards))
    spread_sum = jnp.broadcast_to(run_sum[:, :, None], (seq_count, heads, shards))
    peers_max, peers_sum, peers_out = (
        lax.all_to_all(spread_max, "seq", split_axis=2, concat_axis=2, tiled=True),
        lax.all_to_all(spread_sum, "seq", split_axis=2, concat_axis=2, tiled=True),
        lax.all_to_all(run_out, "seq", split_axis=2, concat_axis=2, tiled=True),
    )
    top = jnp.max(peers_max, axis=2)
    rescale = jnp.exp(peers_max - top[:, :, None])
    totals = jnp.sum(peers_sum * rescale, axis=2)
    grouped = peers_out.reshape(seq_count, heads, shards, share_width)
    shared_latent = jnp.sum(grouped * rescale[:, :, :, None], axis=2)
    local_portion = (shared_latent / totals[:, :, None]).astype(jnp.bfloat16)
    value_slice = jnp.einsum(
        "gre,req->grq", local_portion, value_up_weight, preferred_element_type=jnp.float32
    )
    value_rows = lax.psum(value_slice, "seq").astype(jnp.bfloat16)
    flat_values = value_rows.reshape(seq_count, heads * value_rows.shape[2])
    partial_out = jnp.dot(flat_values, w_out, preferred_element_type=jnp.float32)
    return lax.psum_scatter(partial_out, "mp", scatter_dimension=1, tiled=True).astype(jnp.bfloat16)


def solution(mesh):
    return jax.shard_map(
        local,
        mesh=mesh,
        in_specs=(
            P(("groups", "seq"), None, None),
            P(("groups", "seq"), None),
            P("groups", "mp", None),
            P("groups", "mp", None),
            P("mp", None, "seq"),
            P("mp", "seq", None),
            P("mp", "seq"),
            P("groups", None),
            P("groups"),
        ),
        out_specs=P("groups", ("seq", "mp")),
        check_vma=False,
    )
```

profile of v0, /device:TPU:0, one launch (start us, length us, event | category | flops | bytes accessed | tf_op | source)
XLA Modules:
  0.0 317.1 jit_solution(13368818275387407663)
XLA Ops:
  10.1 1.9 fusion.40
  13.1 36.4 %all_gather.3 = bf16[8,64,512]{1,0,2:T(8,128)(2,1)} all-gather(bf16[8,64,64]{1,0,2:T(8,128)(2,1)S(1)} %copy.63), channel_id=1, replica_groups=mesh['groups'=2,'seq'=8,'mp'=2] {'seq'}, dimensions={2}, use_global_device_ids=true | all-gather | bytes 589824 | tf_op jit(solution)/shard_map/all_gather | solution.py:20
  49.6 2.3 copy.65
  51.9 129.9 %while.18 = (s32[]{:T(128)}, f32[8,64]{0,1:T(8,128)S(1)}, f32[8,64]{0,1:T(8,128)S(1)}, f32[8,64,512]{2,0,1:T(8,128)S(1)}, bf16[8,128]{1,0:T(8,128)(2,1)S(1)}, /*...) while((s32[]{:T(128)}, f32[8,64]{0,1:T(8,128)S(1)}, ...), condition=%wide.region_6.7_spmd.clone, body=%wide.region_2.6_spmd.clone.sunk | while | flops 102681152 | bytes 8056379 | solution.py:88
  56.7 1.5 fusion.90
  58.2 1.8 fusion.91
  62.0 1.4 fusion.86
  64.8 1.5 fusion.90
  66.3 1.8 fusion.91
  70.2 1.4 fusion.86
  72.9 1.5 fusion.90
  74.5 1.8 fusion.91
  78.3 1.4 fusion.86
  81.0 1.5 fusion.90
  82.6 1.8 fusion.91
  86.4 1.4 fusion.86
  89.2 1.5 fusion.90
  90.7 1.8 fusion.91
  94.5 1.4 fusion.86
  97.3 1.5 fusion.90
  98.8 1.8 fusion.91
  102.6 1.4 fusion.86
  105.4 1.5 fusion.90
  106.9 1.8 fusion.91
  110.7 1.4 fusion.86
  113.5 1.5 fusion.90
  115.0 1.8 fusion.91
  118.9 1.4 fusion.86
  121.6 1.5 fusion.90
  123.2 1.8 fusion.91
  127.0 1.4 fusion.86
  129.8 1.5 fusion.90
  131.3 1.8 fusion.91
  135.1 1.4 fusion.86
  137.9 1.5 fusion.90
  139.4 1.8 fusion.91
  143.2 1.4 fusion.86
  146.0 1.5 fusion.90
  147.5 1.8 fusion.91
  154.1 1.5 fusion.90
  155.6 1.8 fusion.91
  159.5 1.4 fusion.86
  162.2 1.5 fusion.90
  163.7 1.8 fusion.91
  170.3 1.5 fusion.90
  171.9 1.8 fusion.91
  178.5 1.5 fusion.90
  180.0 1.8 fusion.91
  182.5 5.3 %all-to-all-start.2 = ((f32[8,1,512]{2,1,0:T(1,128)}), f32[8,1,512]{2,1,0:T(1,128)S(1)}, u32[]{:S(2)}, u32[]{:S(2)}) async-start(f32[8,1,512]{2,1,0:T(1,128)} %reshape.112), calls=%async_computation.2 | async-start | bytes 32768 | tf_op jit(solution)/shard_map/all_to_all | solution.py:95
  188.6 5.8 %all-to-all-done.2 = f32[8,1,512]{2,1,0:T(1,128)S(1)} async-done(((f32[8,1,512]{2,1,0:T(1,128)}), f32[8,1,512]{2,1,0:T(1,128)S(1)}, u32[]{:S(2)}, u32[]{:S(2)}) %all-to-all-start.2) | async-done | bytes 16416 | tf_op jit(solution)/shard_map/all_to_all | solution.py:95
  194.4 3.3 %all-to-all-start.1 = ((f32[8,1,512]{2,1,0:T(1,128)}), f32[8,1,512]{2,1,0:T(1,128)S(1)}, u32[]{:S(2)}, u32[]{:S(2)}) async-start(f32[8,1,512]{2,1,0:T(1,128)} %reshape.110), calls=%async_computation.1 | async-start | bytes 32768 | tf_op jit(solution)/shard_map/all_to_all | solution.py:94
  197.8 2.3 copy.67
  200.1 3.4 %reshape.108 = f32[8,1,32768]{2,1,0:T(1,128)} reshape(f32[512,8,64]{2,1,0:T(8,128)} %bitcast.64) | data formatting | bytes 2097152
  204.4 5.0 %all-to-all-start = ((f32[8,1,32768]{2,1,0:T(1,128)}), f32[8,1,32768]{2,1,0:T(1,128)S(1)}, u32[]{:S(2)}, u32[]{:S(2)}) async-start(f32[8,1,32768]{2,1,0:T(1,128)} %reshape.108), calls=%async_computation | async-start | bytes 2097152 | tf_op jit(solution)/shard_map/all_to_all | solution.py:96
  211.9 16.0 %all-to-all-done = f32[8,1,32768]{2,1,0:T(1,128)S(1)} async-done(((f32[8,1,32768]{2,1,0:T(1,128)}), f32[8,1,32768]{2,1,0:T(1,128)S(1)}, u32[]{:S(2)}, u32[]{:S(2)}) %all-to-all-start) | async-done | bytes 1048608 | tf_op jit(solution)/shard_map/all_to_all | solution.py:96
  227.9 3.1 reduce
  231.0 2.2 reshape.109
  233.2 9.4 %copy.70 = f32[8,64,8,64]{0,1,3,2:T(8,128)} copy(f32[8,64,8,64]{1,0,3,2:T(8,128)} %bitcast.63) | data formatting | bytes 2097152 | tf_op jit(solution)/shard_map/reshape | solution.py:101
  242.6 9.7 %multiply_reduce_fusion = f32[8,64,64]{0,1,2:T(8,128)} fusion(f32[8,64,8,64]{0,1,3,2:T(8,128)} %copy.70, f32[8,64,8]{0,1,2:T(8,128)S(1)} %copy.69), kind=kLoop, calls=%fused_computation.53 | loop fusion | flops 491520 | bytes 1196032 | tf_op jit(solution)/shard_map/reduce_sum | solution.py:102
  252.3 2.7 copy.72
  255.5 38.2 %all-reduce.1 = bf16[8,64,128]{2,0,1:T(8,128)(2,1)S(1)} all-reduce(f32[8,64,128]{2,0,1:T(8,128)S(1)} %convolution_bitcast_fusion.2), channel_id=1, replica_groups=mesh['groups'=2,'seq'=8,'mp'=2] {'seq'}, use_global_device_ids=true, to_apply=%region_10.11 | all-reduce | flops 65536 | bytes 393216 | tf_op jit(solution)/shard_map/psum | solution.py:107
  293.8 9.8 %convolution_bitcast_fusion.1 = f32[896,8]{1,0:T(8,128)} fusion(bf16[8192,896]{1,0:T(8,128)(2,1)} %param.17, bf16[8,64,128]{2,0,1:T(8,128)(2,1)S(1)} %all-reduce.1), kind=kOutput, calls=%fused_computation.54 | convolution fusion | flops 117440512 | bytes 14839808
  303.6 5.1 %reduce-scatter.4.cloned.1.call-done = f32[448,8]{1,0:T(8,128)} async-done(((f32[896,8]{1,0:T(8,128)}), f32[448,8]{1,0:T(8,128)}) %reduce-scatter.4.cloned.1.call-update) | async-done | bytes 14352
  308.6 1.6 copy.78
  (341 shorter events, 69.2 us)
Async XLA Ops:
  6.5 248.6 %copy-start = (bf16[64,64,128]{2,1,0:T(8,128)(2,1)S(1)}, bf16[64,64,128]{2,1,0:T(8,128)(2,1)}, u32[]{:S(2)}) copy-start(bf16[64,64,128]{2,1,0:T(8,128)(2,1)} %param.16) | copy-start | bytes 3145732
  182.5 11.9 %all-to-all-start.2 = ((f32[8,1,512]{2,1,0:T(1,128)}), f32[8,1,512]{2,1,0:T(1,128)S(1)}, u32[]{:S(2)}, u32[]{:S(2)}) async-start(f32[8,1,512]{2,1,0:T(1,128)} %reshape.112), calls=%async_computation.2 | async-start | bytes 32768 | tf_op jit(solution)/shard_map/all_to_all | solution.py:95
  194.4 9.9 %all-to-all-start.1 = ((f32[8,1,512]{2,1,0:T(1,128)}), f32[8,1,512]{2,1,0:T(1,128)S(1)}, u32[]{:S(2)}, u32[]{:S(2)}) async-start(f32[8,1,512]{2,1,0:T(1,128)} %reshape.110), calls=%async_computation.1 | async-start | bytes 32768 | tf_op jit(solution)/shard_map/all_to_all | solution.py:94
  204.4 23.5 %all-to-all-start = ((f32[8,1,32768]{2,1,0:T(1,128)}), f32[8,1,32768]{2,1,0:T(1,128)S(1)}, u32[]{:S(2)}, u32[]{:S(2)}) async-start(f32[8,1,32768]{2,1,0:T(1,128)} %reshape.108), calls=%async_computation | async-start | bytes 2097152 | tf_op jit(solution)/shard_map/all_to_all | solution.py:96
  209.4 99.2 %reduce-scatter.4.cloned.1.call-start = ((), (), s32[]{:S(2)}) async-start(), calls=%async_computation.4 | async-start | bytes 688128
Sparse Core Ops, SparseCore 0:
  303.7 4.9 reduce-scatter.3
where the time goes:
time: 320 us; the launch traced here: 317 us
  matrix products  110 us (34%)
  blocking collectives  74.7 us (23%)
  local copies, waits for them, and re-layouts  51.6 us (16%)
  waiting for transfers between devices  27.9 us (9%)
  other arithmetic  24.3 us (8%)
  starting transfers between devices  13.9 us (4%)
  between operations  13.5 us (4%)
    psum x1, blocking collectives, local(): value_rows = lax.psum(value_slice, 'seq').astype(jnp.bfloat16)  38.2 us
    all_gather x1, blocking collectives, local(): q_latent = lax.all_gather(q_part, 'seq', axis=2, tiled=True)  36.4 us
    dot_general x16, matrix products, update(): jnp.einsum('bsh,shk->bhk', factor, slot_out, precision=peak_score)  28.3 us
    dot_general x16, matrix products, update(): jnp.einsum('sht,stk->shk', exponent.astype(jnp.bfloat16), latent_block, p...  24.3 us
    dot_general x16, matrix products, update(): jnp.einsum('shk,stk->sht', pick_latent, latent_block, preferred_element_t...  22 us
    all_to_all x1, waiting for transfers between devices, local(): lax.all_to_all(run_out, 'seq', split_axis=2, concat_axis=2, tiled=True)  16 us
    dynamic_slice x16, local copies, waits for them, and re-layouts, update(): lax.dynamic_slice_in_dim(rope_cache, start, 8, 0)  13.5 us
    unnamed x13, local copies, waits for them, and re-layouts  12 us
  transfers between devices with their start and end apart: 4, of which 4 were waited for; matrix products, arithmetic and copies ran while one was open for 3% of the time, Pallas kernels for 0%

commit v1 on v0

--- a/solution.py
+++ b/solution.py
@@ -4,6 +4,15 @@
 from jax.sharding import PartitionSpec as P
 
 NEG = -1e30
+point_the_grid = lambda dim_at, pos_dim, z: jnp.concatenate(
+    lax.all_to_all(
+        jnp.stack(jnp.split(z, lax.axis_size("seq"), axis=dim_at)),
+        "seq",
+        split_axis=0,
+        concat_axis=0,
+    ),
+    axis=pos_dim,
+)
 
 
 def local(
@@ -93,7 +102,7 @@
     peers_max, peers_sum, peers_out = (
         lax.all_to_all(spread_max, "seq", split_axis=2, concat_axis=2, tiled=True),
         lax.all_to_all(spread_sum, "seq", split_axis=2, concat_axis=2, tiled=True),
-        lax.all_to_all(run_out, "seq", split_axis=2, concat_axis=2, tiled=True),
+        point_the_grid(2, 2, run_out),
     )
     top = jnp.max(peers_max, axis=2)
     rescale = jnp.exp(peers_max - top[:, :, None])

time: 320 us -> 354 us (1.11)
  matrix products: 110 us -> 141 us
  other arithmetic: 24.3 us -> 37.5 us
  local copies, waits for them, and re-layouts: 51.6 us -> 43.2 us
    add x16, other arithmetic: 0.36 us -> 21.4 us  [update(): run_sum * carry_scale]
    dot_general x16, matrix products: 5.57 us -> 22.2 us  [update(): jnp.einsum('bs,bhk->shk', owner_block, q_latent, preferred_element_type=j...]
    dot_general x16, matrix products: 3.62 us -> 18.3 us  [update(): jnp.einsum('bs,bhr->shr', owner_block, q_rope, preferred_element_type=jnp...]
    reshape x1 -> x0, local copies, waits for them, and re-layouts: 9.39 us -> none  [local(): grouped = peers_out.reshape(seq_count, heads, shards, share_width)]
    reduce_sum x1, other arithmetic: 9.67 us -> 1.94 us  [local(): shared_latent = jnp.sum(grouped * rescale[:, :, :, None], axis=2)]
    unnamed x13 -> x24, local copies, waits for them, and re-layouts: 12 us -> 17 us
  transfers between devices with their start and end apart: 4 -> 4, of which waited for: 4 -> 4; matrix products, arithmetic and copies ran while one was open for 3% -> 4% of each run, Pallas kernels for 0% -> 0%
where the time goes in v1:
time: 354 us; the launch traced here: 349 us
  matrix products  141 us (40%)
  blocking collectives  72.8 us (21%)
  local copies, waits for them, and re-layouts  43.2 us (12%)
  other arithmetic  37.5 us (11%)
  waiting for transfers between devices  24.8 us (7%)
  starting transfers between devices  14.8 us (4%)
  between operations  13.5 us (4%)
    psum x1, blocking collectives, local(): value_rows = lax.psum(value_slice, 'seq').astype(jnp.bfloat16)  38.2 us
    all_gather x1, blocking collectives, local(): q_latent = lax.all_gather(q_part, 'seq', axis=2, tiled=True)  34.6 us
    dot_general x16, matrix products, update(): jnp.einsum('bsh,shk->bhk', factor, slot_out, precision=peak_score)  28.3 us
    dot_general x16, matrix products, update(): jnp.einsum('sht,stk->shk', exponent.astype(jnp.bfloat16), latent_block, p...  24.3 us
    dot_general x16, matrix products, update(): jnp.einsum('bs,bhk->shk', owner_block, q_latent, preferred_element_type=j...  22.2 us
    dot_general x16, matrix products, update(): jnp.einsum('shk,stk->sht', pick_latent, latent_block, preferred_element_t...  22 us
    add x16, other arithmetic, update(): run_sum * carry_scale  21.4 us
    dot_general x16, matrix products, update(): jnp.einsum('bs,bhr->shr', owner_block, q_rope, preferred_element_type=jnp...  18.3 us
  transfers between devices with their start and end apart: 4, of which 4 were waited for; matrix products, arithmetic and copies ran while one was open for 4% of the time, Pallas kernels for 0%

profile of v1, /device:TPU:0, one launch (start us, length us, event | category | flops | bytes accessed | tf_op | source)
XLA Modules:
  0.0 349.3 jit_solution(11930661633004383327)
XLA Ops:
  10.1 1.9 fusion.41
  12.2 34.6 %all_gather.3 = bf16[8,64,512]{1,0,2:T(8,128)(2,1)S(1)} all-gather(bf16[8,64,64]{1,0,2:T(8,128)(2,1)S(1)} %copy.41), channel_id=1, replica_groups=mesh['groups'=2,'seq'=8,'mp'=2] {'seq'}, dimensions={2}, use_global_device_ids=true | all-gather | bytes 589824 | tf_op jit(solution)/shard_map/all_gather | solution.py:29
  46.8 2.0 copy.43
  49.5 182.4 %while.18 = (s32[]{:T(128)}, f32[8,64]{0,1:T(8,128)S(1)}, f32[8,64]{0,1:T(8,128)}, f32[8,64,512]{2,0,1:T(8,128)S(1)}, bf16[8,128]{1,0:T(8,128)(2,1)S(1)}, /*inde...) while((s32[]{:T(128)}, f32[8,64]{0,1:T(8,128)S(1)}, ...), condition=%wide.region_6.7_spmd.clone, body=%wide.region_2.6_spmd.clone.sunk | while | flops 102681152 | bytes 8060523 | solution.py:97
  49.6 1.4 convolution_convert_fusion.5
  55.0 1.5 fusion.91
  58.4 1.8 fusion.92
  60.3 1.4 convolution_convert_fusion.5
  65.7 1.5 fusion.91
  69.9 1.8 fusion.92
  71.8 1.4 convolution_convert_fusion.5
  77.1 1.5 fusion.91
  81.3 1.8 fusion.92
  83.2 1.4 convolution_convert_fusion.5
  88.6 1.5 fusion.91
  92.8 1.8 fusion.92
  94.7 1.4 convolution_convert_fusion.5
  100.0 1.5 fusion.91
  104.2 1.8 fusion.92
  106.1 1.4 convolution_convert_fusion.5
  111.5 1.5 fusion.91
  115.7 1.8 fusion.92
  117.6 1.4 convolution_convert_fusion.5
  122.9 1.5 fusion.91
  127.1 1.8 fusion.92
  129.0 1.4 convolution_convert_fusion.5
  134.3 1.5 fusion.91
  138.6 1.8 fusion.92
  140.5 1.4 convolution_convert_fusion.5
  145.8 1.5 fusion.91
  150.0 1.8 fusion.92
  151.9 1.4 convolution_convert_fusion.5
  157.2 1.5 fusion.91
  161.5 1.8 fusion.92
  163.4 1.4 convolution_convert_fusion.5
  168.7 1.5 fusion.91
  172.9 1.8 fusion.92
  174.8 1.4 convolution_convert_fusion.5
  180.1 1.5 fusion.91
  184.4 1.8 fusion.92
  186.3 1.4 convolution_convert_fusion.5
  191.6 1.5 fusion.91
  195.8 1.8 fusion.92
  197.7 1.4 convolution_convert_fusion.5
  203.0 1.5 fusion.91
  207.3 1.8 fusion.92
  214.5 1.5 fusion.91
  218.7 1.8 fusion.92
  220.6 1.4 convolution_convert_fusion.5
  225.9 1.5 fusion.91
  230.2 1.8 fusion.92
  232.7 5.4 %all-to-all-start.1 = ((f32[8,1,512]{2,1,0:T(1,128)}), f32[8,1,512]{2,1,0:T(1,128)S(1)}, u32[]{:S(2)}, u32[]{:S(2)}) async-start(f32[8,1,512]{2,1,0:T(1,128)} %reshape.110), calls=%async_computation.1 | async-start | bytes 32768 | tf_op jit(solution)/shard_map/all_to_all | solution.py:103
  244.7 5.7 %all-to-all-start.2 = ((f32[8,1,512]{2,1,0:T(1,128)}), f32[8,1,512]{2,1,0:T(1,128)S(1)}, u32[]{:S(2)}, u32[]{:S(2)}) async-start(f32[8,1,512]{2,1,0:T(1,128)} %reshape.112), calls=%async_computation.2 | async-start | bytes 32768 | tf_op jit(solution)/shard_map/all_to_all | solution.py:104
  251.2 3.4 reshape.108
  254.6 2.5 all-to-all-done.2
  257.0 3.6 %all-to-all-start = ((f32[8,1,32768]{2,1,0:T(1,128)}), f32[8,1,32768]{2,1,0:T(1,128)S(1)}, u32[]{:S(2)}, u32[]{:S(2)}) async-start(f32[8,1,32768]{2,1,0:T(1,128)} %reshape.108), calls=%async_computation | async-start | bytes 2097152 | tf_op jit(solution)/shard_map/all_to_all | solution.py:8
  263.1 16.7 %all-to-all-done = f32[8,1,32768]{2,1,0:T(1,128)S(1)} async-done(((f32[8,1,32768]{2,1,0:T(1,128)}), f32[8,1,32768]{2,1,0:T(1,128)S(1)}, u32[]{:S(2)}, u32[]{:S(2)}) %all-to-all-start) | async-done | bytes 1048608 | tf_op jit(solution)/shard_map/all_to_all | solution.py:8
  279.9 3.1 reduce.2
  283.0 2.2 reshape.109
  285.2 1.9 fusion.40
  287.6 38.2 %all-reduce.1 = bf16[8,64,128]{2,0,1:T(8,128)(2,1)S(1)} all-reduce(f32[8,64,128]{2,0,1:T(8,128)S(1)} %convolution_bitcast_fusion.2), channel_id=1, replica_groups=mesh['groups'=2,'seq'=8,'mp'=2] {'seq'}, use_global_device_ids=true, to_apply=%region_10.11 | all-reduce | flops 65536 | bytes 393216 | tf_op jit(solution)/shard_map/psum | solution.py:116
  325.8 9.8 %convolution_bitcast_fusion.1 = f32[896,8]{1,0:T(8,128)} fusion(bf16[8192,896]{1,0:T(8,128)(2,1)} %param.17, bf16[8,64,128]{2,0,1:T(8,128)(2,1)S(1)} %all-reduce.1), kind=kOutput, calls=%fused_computation.55 | convolution fusion | flops 117440512 | bytes 14839808
  335.6 5.2 %reduce-scatter.4.cloned.1.call-done = f32[448,8]{1,0:T(8,128)} async-done(((f32[896,8]{1,0:T(8,128)}), f32[448,8]{1,0:T(8,128)}) %reduce-scatter.4.cloned.1.call-update) | async-done | bytes 14352
  340.8 1.6 copy.53
  (414 shorter events, 122.6 us)
Async XLA Ops:
  6.5 280.6 %copy-start = (bf16[64,64,128]{2,1,0:T(8,128)(2,1)S(1)}, bf16[64,64,128]{2,1,0:T(8,128)(2,1)}, u32[]{:S(2)}) copy-start(bf16[64,64,128]{2,1,0:T(8,128)(2,1)} %param.16) | copy-start | bytes 3145732
  10.1 38.7 %copy-start.2 = (bf16[8,64,64]{2,1,0:T(8,128)(2,1)S(1)}, bf16[8,64,64]{2,1,0:T(8,128)(2,1)}, u32[]{:S(2)}) copy-start(bf16[8,64,64]{2,1,0:T(8,128)(2,1)} %param.14) | copy-start | bytes 196612
  49.5 5.0 %copy-start.3 = (s32[128]{0:T(128)}, s32[128]{0:T(128)S(1)}, u32[]{:S(2)}) copy-start(s32[128]{0:T(128)S(1)} %get-tuple-element.382) | copy-start | bytes 1540 | tf_op jit(solution)/shard_map/while
  57.1 3.1 copy-start.4
  60.2 5.0 %copy-start.3 = (s32[128]{0:T(128)}, s32[128]{0:T(128)S(1)}, u32[]{:S(2)}) copy-start(s32[128]{0:T(128)S(1)} %get-tuple-element.382) | copy-start | bytes 1540 | tf_op jit(solution)/shard_map/while
  67.8 3.9 %copy-start.4 = (s32[128]{0:T(128)S(1)}, s32[128]{0:T(128)}, u32[]{:S(2)}) copy-start(s32[128]{0:T(128)} %copy-done.3) | copy-start | bytes 1540 | tf_op jit(solution)/shard_map/while
  71.7 5.0 %copy-start.3 = (s32[128]{0:T(128)}, s32[128]{0:T(128)S(1)}, u32[]{:S(2)}) copy-start(s32[128]{0:T(128)S(1)} %get-tuple-element.382) | copy-start | bytes 1540 | tf_op jit(solution)/shard_map/while
  79.2 3.9 %copy-start.4 = (s32[128]{0:T(128)S(1)}, s32[128]{0:T(128)}, u32[]{:S(2)}) copy-start(s32[128]{0:T(128)} %copy-done.3) | copy-start | bytes 1540 | tf_op jit(solution)/shard_map/while
  83.1 5.0 %copy-start.3 = (s32[128]{0:T(128)}, s32[128]{0:T(128)S(1)}, u32[]{:S(2)}) copy-start(s32[128]{0:T(128)S(1)} %get-tuple-element.382) | copy-start | bytes 1540 | tf_op jit(solution)/shard_map/while
  90.7 3.9 %copy-start.4 = (s32[128]{0:T(128)S(1)}, s32[128]{0:T(128)}, u32[]{:S(2)}) copy-start(s32[128]{0:T(128)} %copy-done.3) | copy-start | bytes 1540 | tf_op jit(solution)/shard_map/while
  94.6 5.0 %copy-start.3 = (s32[128]{0:T(128)}, s32[128]{0:T(128)S(1)}, u32[]{:S(2)}) copy-start(s32[128]{0:T(128)S(1)} %get-tuple-element.382) | copy-start | bytes 1540 | tf_op jit(solution)/shard_map/while
  102.1 3.9 %copy-start.4 = (s32[128]{0:T(128)S(1)}, s32[128]{0:T(128)}, u32[]{:S(2)}) copy-start(s32[128]{0:T(128)} %copy-done.3) | copy-start | bytes 1540 | tf_op jit(solution)/shard_map/while
  106.0 5.0 %copy-start.3 = (s32[128]{0:T(128)}, s32[128]{0:T(128)S(1)}, u32[]{:S(2)}) copy-start(s32[128]{0:T(128)S(1)} %get-tuple-element.382) | copy-start | bytes 1540 | tf_op jit(solution)/shard_map/while
  113.6 3.9 %copy-start.4 = (s32[128]{0:T(128)S(1)}, s32[128]{0:T(128)}, u32[]{:S(2)}) copy-start(s32[128]{0:T(128)} %copy-done.3) | copy-start | bytes 1540 | tf_op jit(solution)/shard_map/while
  117.5 5.0 %copy-start.3 = (s32[128]{0:T(128)}, s32[128]{0:T(128)S(1)}, u32[]{:S(2)}) copy-start(s32[128]{0:T(128)S(1)} %get-tuple-element.382) | copy-start | bytes 1540 | tf_op jit(solution)/shard_map/while
  125.0 3.9 %copy-start.4 = (s32[128]{0:T(128)S(1)}, s32[128]{0:T(128)}, u32[]{:S(2)}) copy-start(s32[128]{0:T(128)} %copy-done.3) | copy-start | bytes 1540 | tf_op jit(solution)/shard_map/while
  128.9 5.0 %copy-start.3 = (s32[128]{0:T(128)}, s32[128]{0:T(128)S(1)}, u32[]{:S(2)}) copy-start(s32[128]{0:T(128)S(1)} %get-tuple-element.382) | copy-start | bytes 1540 | tf_op jit(solution)/shard_map/while
  136.5 3.9 %copy-start.4 = (s32[128]{0:T(128)S(1)}, s32[128]{0:T(128)}, u32[]{:S(2)}) copy-start(s32[128]{0:T(128)} %copy-done.3) | copy-start | bytes 1540 | tf_op jit(solution)/shard_map/while
  140.4 5.0 %copy-start.3 = (s32[128]{0:T(128)}, s32[128]{0:T(128)S(1)}, u32[]{:S(2)}) copy-start(s32[128]{0:T(128)S(1)} %get-tuple-element.382) | copy-start | bytes 1540 | tf_op jit(solution)/shard_map/while
  147.9 3.9 %copy-start.4 = (s32[128]{0:T(128)S(1)}, s32[128]{0:T(128)}, u32[]{:S(2)}) copy-start(s32[128]{0:T(128)} %copy-done.3) | copy-start | bytes 1540 | tf_op jit(solution)/shard_map/while
  151.8 5.0 %copy-start.3 = (s32[128]{0:T(128)}, s32[128]{0:T(128)S(1)}, u32[]{:S(2)}) copy-start(s32[128]{0:T(128)S(1)} %get-tuple-element.382) | copy-start | bytes 1540 | tf_op jit(solution)/shard_map/while
  159.4 3.9 %copy-start.4 = (s32[128]{0:T(128)S(1)}, s32[128]{0:T(128)}, u32[]{:S(2)}) copy-start(s32[128]{0:T(128)} %copy-done.3) | copy-start | bytes 1540 | tf_op jit(solution)/shard_map/while
  163.3 5.0 %copy-start.3 = (s32[128]{0:T(128)}, s32[128]{0:T(128)S(1)}, u32[]{:S(2)}) copy-start(s32[128]{0:T(128)S(1)} %get-tuple-element.382) | copy-start | bytes 1540 | tf_op jit(solution)/shard_map/while
  170.8 3.9 %copy-start.4 = (s32[128]{0:T(128)S(1)}, s32[128]{0:T(128)}, u32[]{:S(2)}) copy-start(s32[128]{0:T(128)} %copy-done.3) | copy-start | bytes 1540 | tf_op jit(solution)/shard_map/while
  174.7 5.0 %copy-start.3 = (s32[128]{0:T(128)}, s32[128]{0:T(128)S(1)}, u32[]{:S(2)}) copy-start(s32[128]{0:T(128)S(1)} %get-tuple-element.382) | copy-start | bytes 1540 | tf_op jit(solution)/shard_map/while
  182.3 3.9 %copy-start.4 = (s32[128]{0:T(128)S(1)}, s32[128]{0:T(128)}, u32[]{:S(2)}) copy-start(s32[128]{0:T(128)} %copy-done.3) | copy-start | bytes 1540 | tf_op jit(solution)/shard_map/while
  186.2 5.0 %copy-start.3 = (s32[128]{0:T(128)}, s32[128]{0:T(128)S(1)}, u32[]{:S(2)}) copy-start(s32[128]{0:T(128)S(1)} %get-tuple-element.382) | copy-start | bytes 1540 | tf_op jit(solution)/shard_map/while
  193.7 3.9 %copy-start.4 = (s32[128]{0:T(128)S(1)}, s32[128]{0:T(128)}, u32[]{:S(2)}) copy-start(s32[128]{0:T(128)} %copy-done.3) | copy-start | bytes 1540 | tf_op jit(solution)/shard_map/while
  197.6 5.0 %copy-start.3 = (s32[128]{0:T(128)}, s32[128]{0:T(128)S(1)}, u32[]{:S(2)}) copy-start(s32[128]{0:T(128)S(1)} %get-tuple-element.382) | copy-start | bytes 1540 | tf_op jit(solution)/shard_map/while
  205.1 3.9 %copy-start.4 = (s32[128]{0:T(128)S(1)}, s32[128]{0:T(128)}, u32[]{:S(2)}) copy-start(s32[128]{0:T(128)} %copy-done.3) | copy-start | bytes 1540 | tf_op jit(solution)/shard_map/while
  209.1 5.0 %copy-start.3 = (s32[128]{0:T(128)}, s32[128]{0:T(128)S(1)}, u32[]{:S(2)}) copy-start(s32[128]{0:T(128)S(1)} %get-tuple-element.382) | copy-start | bytes 1540 | tf_op jit(solution)/shard_map/while
  216.6 3.9 %copy-start.4 = (s32[128]{0:T(128)S(1)}, s32[128]{0:T(128)}, u32[]{:S(2)}) copy-start(s32[128]{0:T(128)} %copy-done.3) | copy-start | bytes 1540 | tf_op jit(solution)/shard_map/while
  220.5 5.0 %copy-start.3 = (s32[128]{0:T(128)}, s32[128]{0:T(128)S(1)}, u32[]{:S(2)}) copy-start(s32[128]{0:T(128)S(1)} %get-tuple-element.382) | copy-start | bytes 1540 | tf_op jit(solution)/shard_map/while
  228.0 3.9 %copy-start.4 = (s32[128]{0:T(128)S(1)}, s32[128]{0:T(128)}, u32[]{:S(2)}) copy-start(s32[128]{0:T(128)} %copy-done.3) | copy-start | bytes 1540 | tf_op jit(solution)/shard_map/while
  232.0 11.6 %copy-start.1 = (f32[8,64]{0,1:T(8,128)S(1)}, f32[8,64]{0,1:T(8,128)}, u32[]{:S(2)}) copy-start(f32[8,64]{0,1:T(8,128)} %get-tuple-element.178) | copy-start | bytes 6148
  232.7 11.9 %all-to-all-start.1 = ((f32[8,1,512]{2,1,0:T(1,128)}), f32[8,1,512]{2,1,0:T(1,128)S(1)}, u32[]{:S(2)}, u32[]{:S(2)}) async-start(f32[8,1,512]{2,1,0:T(1,128)} %reshape.110), calls=%async_computation.1 | async-start | bytes 32768 | tf_op jit(solution)/shard_map/all_to_all | solution.py:103
  244.7 12.4 %all-to-all-start.2 = ((f32[8,1,512]{2,1,0:T(1,128)}), f32[8,1,512]{2,1,0:T(1,128)S(1)}, u32[]{:S(2)}, u32[]{:S(2)}) async-start(f32[8,1,512]{2,1,0:T(1,128)} %reshape.112), calls=%async_computation.2 | async-start | bytes 32768 | tf_op jit(solution)/shard_map/all_to_all | solution.py:104
  257.0 22.8 %all-to-all-start = ((f32[8,1,32768]{2,1,0:T(1,128)}), f32[8,1,32768]{2,1,0:T(1,128)S(1)}, u32[]{:S(2)}, u32[]{:S(2)}) async-start(f32[8,1,32768]{2,1,0:T(1,128)} %reshape.108), calls=%async_computation | async-start | bytes 2097152 | tf_op jit(solution)/shard_map/all_to_all | solution.py:8
  260.6 80.2 %reduce-scatter.4.cloned.1.call-start = ((), (), s32[]{:S(2)}) async-start(), calls=%async_computation.4 | async-start | bytes 688128
Sparse Core Ops, SparseCore 0:
  335.7 5.0 reduce-scatter.3
